TPU v7x, 32 devices: a whole 2x2x4 slice. The times are simulated.
32 devices in a mesh: dp: 4 (over y, x), group: 8 (over z, core).
Axes of the slice: x: 2, y: 2, z: 4, core: 2. Of those that a mesh axis runs over, the one named last changes fastest.
Arguments:
- tokens: bfloat16 [2048, 5120], P('dp'), may hold values from -6 to 6
- frame_mask: int32 [2048], P('dp'), may hold values 0 or 1
- cotangent: bfloat16 [2048, 5120], P('dp'), may hold values from -0.625 to 0.625
- up_weight: bfloat16 [5120, 8192], P('dp', 'group'), may hold values from -0.078125 to 0.078125
- down_weight: bfloat16 [5120, 8192], P('dp', 'group'), may hold values from -0.0625 to 0.0625
- snap_params: bfloat16 [8, 32768], P(None, ('dp', 'group')), may hold values from -6 to 6
- first_moment: float32 [8, 32768], P(None, ('dp', 'group')), may hold values from -6 to 6
- second_moment: float32 [8, 32768], P(None, ('dp', 'group')), may hold values from 0.01 to 4
- range_of_writer: int32 [8], replicated, may hold values from 0 to 7, each once
Outputs:
- grad_up: float32 [5120, 8192], P('dp', 'group')
- grad_down: float32 [5120, 8192], P('dp', 'group')
- written_params: bfloat16 [8, 32768], P('group', 'dp')
- written_moments: float32 [2, 8, 32768], P(None, 'group', 'dp')
Inputs may be any that keep to these rules, and one draw needn't show every extreme that they name: `range_of_writer`: each of the 8 ranges is named by exactly one owner.
All inputs are finite; a program needn't handle non-finite values. No bound on the sum of `frame_mask` on one device may be relied on, other than what follows from the above.
Results may differ from a plain program's by a relative error of at most 0.017.
Values may be sent and summed in bfloat16 or wider, within the bound.
No kernel may reach another device: no remote copies, remote signals or barrier semaphores. Data moves between devices by JAX's collectives and lax.ppermute only.
A program may use at most 128 MiB of HBM per device.

v0:
```python
import jax
import jax.numpy as jnp
from jax import lax
from jax.sharding import PartitionSpec as P

EPS = 1e-06


def normalize(tokens):
    values = tokens.astype(jnp.float32)
    centred = values - jnp.mean(values, axis=1, keepdims=True)
    spread = jnp.mean(centred * centred, axis=1, keepdims=True)
    return (centred * lax.rsqrt(spread + EPS)).astype(jnp.bfloat16)


def gelu_pair(pre, d_act):
    act, pullback = jax.vjp(lambda v: jax.nn.gelu(v, approximate=True), pre)
    return (act.astype(jnp.bfloat16), pullback(d_act)[0].astype(jnp.bfloat16))


def outer_sum(left, right):
    return lax.dot_general(
        left, right, (((0,), (0,)), ((), ())), preferred_element_type=jnp.float32
    )


def regroup(snap_params, first_moment, second_moment, range_of_writer):
    send_params = jnp.take(snap_params, range_of_writer, axis=0)
    send_first = jnp.take(first_moment, range_of_writer, axis=0)
    send_second = jnp.take(second_moment, range_of_writer, axis=0)
    written_params = lax.all_to_all(send_params, "group", split_axis=0, concat_axis=1, tiled=True)
    got_first, got_second = (
        lax.all_to_all(
            send_first.astype(jnp.bfloat16), "group", split_axis=0, concat_axis=1, tiled=True
        ).astype(send_first.dtype),
        lax.all_to_all(
            send_second.astype(jnp.bfloat16), "group", split_axis=0, concat_axis=1, tiled=True
        ).astype(send_second.dtype),
    )
    return (written_params, jnp.stack([got_first, got_second]))


def per_device(
    tokens,
    frame_mask,
    cotangent,
    up_weight,
    down_weight,
    snap_params,
    first_moment,
    second_moment,
    range_of_writer,
):
    written = regroup(snap_params, first_moment, second_moment, range_of_writer)
    normed = normalize(tokens)
    masked = cotangent * frame_mask[:, None].astype(jnp.bfloat16)
    hidden_cols = up_weight.shape[1]
    left = normed
    right = masked
    pre = jnp.dot(
        left,
        lax.all_gather(up_weight, "dp", axis=0, tiled=True),
        preferred_element_type=jnp.float32,
    )
    d_act = jnp.dot(
        right,
        lax.all_gather(down_weight, "dp", axis=0, tiled=True),
        preferred_element_type=jnp.float32,
    )
    act, grad_pre = gelu_pair(pre, d_act)
    left = normed
    right = masked
    summed = lax.psum_scatter(
        jnp.concatenate([outer_sum(left, grad_pre), outer_sum(right, act)], axis=1).astype(
            jnp.bfloat16
        ),
        "dp",
        scatter_dimension=0,
        tiled=True,
    ).astype(jnp.float32)
    grad_up = summed[:, :hidden_cols]
    grad_down = summed[:, hidden_cols:]
    return (grad_up, grad_down, written[0], written[1])


def solution(mesh):
    placed = (
        P("dp", None),
        P("dp"),
        P("dp", None),
        P("dp", "group"),
        P("dp", "group"),
        P(None, ("dp", "group")),
        P(None, ("dp", "group")),
        P(None, ("dp", "group")),
        P(),
    )
    return jax.shard_map(
        per_device,
        mesh=mesh,
        in_specs=placed,
        out_specs=(P("dp", "group"), P("dp", "group"), P("group", "dp"), P(None, "group", "dp")),
        check_vma=False,
    )
```

profile of v0, /device:TPU:0, one launch (start us, length us, event | category | flops | bytes accessed | tf_op | source)
XLA Modules:
  0.0 468.0 jit_solution(11517369713372826682)
XLA Ops:
  7.2 0.0 copy-start
  7.2 0.0 copy-start.4
  7.2 0.0 all-gather.5.cloned.1.call-start
  7.2 0.7 all-gather.5.cloned.1.call-update
  7.9 0.0 all-gather.3.cloned.1.call-start
  8.0 0.7 all-gather.3.cloned.1.call-update
  8.7 0.0 reduce-scatter.2.cloned.1.call-start
  8.7 0.0 copy-done.4
  8.7 0.0 copy-start.1
  8.8 3.4 convert_reduce_fusion
  12.2 0.6 copy-done.1
  12.8 1.5 fusion.2
  14.3 103.2 %all-gather.5.cloned.1.call-done = bf16[5120,1024]{1,0:T(8,128)(2,1)} async-done(((bf16[1280,1024]{1,0:T(8,128)(2,1)}), bf16[5120,1024]{1,0:T(8,128)(2,1)}) %all-gather.5.cloned.1.call-update) | async-done | bytes 10485776 | tf_op jit(solution)/shard_map/all_gather | solution.py:62
  117.5 9.9 %fusion.29 = f32[512,1024]{1,0:T(8,128)S(1)} fusion(bf16[5120,1024]{1,0:T(8,128)(2,1)} %all-gather.5.cloned.1.call-done, bf16[512,5120]{1,0:T(8,128)(2,1)} %param.11, f32[512]{0:T(512)S(1)} %add_rsqrt_fusion, f32[512]{0:T(512)S(1)} %broadcast_multiply_fusion), kind=kOutput, calls=%fused_computation.46 | convolution fusion | flops 5379194880 | bytes 17829888 | tf_op jit(solution)/shard_map/dot_general | solution.py:60
  127.5 11.7 %convolution_convert_fusion = bf16[5120,1024]{0,1:T(8,128)(2,1)} fusion(bf16[512,5120]{1,0:T(8,128)(2,1)} %param.13, bf16[512]{0:T(512)(128)(2,1)S(1)} %convert_element_type.54, f32[512,1024]{1,0:T(8,128)S(1)} %fusion.29), kind=kOutput, calls=%fused_computation.10 | convolution fusion | flops 5381292032 | bytes 17826816 | tf_op jit(solution)/shard_map/dot_general | solution.py:22
  139.1 85.2 %all-gather.3.cloned.1.call-done = bf16[5120,1024]{1,0:T(8,128)(2,1)} async-done(((bf16[1280,1024]{1,0:T(8,128)(2,1)}), bf16[5120,1024]{1,0:T(8,128)(2,1)}) %all-gather.3.cloned.1.call-update) | async-done | bytes 10485776 | tf_op jit(solution)/shard_map/all_gather | solution.py:67
  224.3 0.0 slice-start
  224.3 0.0 slice-start.1
  224.3 11.9 %fusion.15 = bf16[512,1024]{1,0:T(8,128)(2,1)S(1)} fusion(f32[512,1024]{1,0:T(8,128)S(1)} %fusion.29, bf16[5120,1024]{1,0:T(8,128)(2,1)} %all-gather.3.cloned.1.call-done, bf16[512,5120]{1,0:T(8,128)(2,1)} %param.13, bf16[512]{0:T(512)(128)(2,1)S(1)} %convert_element_type.54), kind=kOutput, calls=%fused_computation.25 | convolution fusion | flops 5381816320 | bytes 18875392 | tf_op jit(solution)/shard_map/dot_general | solution.py:65
  236.2 0.0 slice-start.2
  236.2 9.0 %convolution_convert_fusion.1 = bf16[5120,1024]{0,1:T(8,128)(2,1)S(1)} fusion(bf16[512,1024]{1,0:T(8,128)(2,1)S(1)} %fusion.15, bf16[512,5120]{1,0:T(8,128)(2,1)} %param.11, f32[512]{0:T(512)S(1)} %add_rsqrt_fusion, f32[512]{0:T(512)S(1)} %broadcast_multiply_fusion), kind=kOutput, calls=%fused_computation.11 | convolution fusion | flops 5384437760 | bytes 16781312 | tf_op jit(solution)/shard_map/dot_general | solution.py:22
  245.2 0.0 slice-done
  245.2 0.0 slice-done.1
  245.3 0.0 slice-done.2
  245.3 9.1 %pad_maximum_fusion = bf16[5120,2048]{0,1:T(8,128)(2,1)} fusion(bf16[5120,1024]{0,1:T(8,128)(2,1)S(1)} %bitcast.13, bf16[5120,1024]{0,1:T(8,128)(2,1)S(1)} %convolution_convert_fusion.1), kind=kLoop, calls=%fused_computation.3 | loop fusion | flops 41943040 | bytes 41943040 | tf_op jit(solution)/shard_map/concatenate | solution.py:74
  254.4 0.0 copy-start.5
  254.4 0.0 copy-start.3
  254.4 0.0 copy-start.2
  254.4 0.0 reduce-scatter.2.cloned.1.call-update
  254.4 0.6 copy-done.5
  255.0 0.0 copy-done
  255.0 0.6 gather_fusion.1
  255.6 0.0 copy-done.3
  255.6 0.6 gather_fusion.2
  256.2 0.1 fusion.22
  256.3 0.5 broadcast.123
  256.8 0.7 reduce.2
  257.5 0.6 reshape.139
  258.1 4.6 all-to-all-start.1
  262.7 0.7 reduce.1
  263.3 0.6 reshape.137
  264.0 0.0 copy-done.2
  264.0 0.6 gather_fusion
  264.5 3.8 all-to-all-done.1
  268.3 3.3 all-to-all-start.2
  271.7 0.1 bitcast_select_fusion
  271.8 0.7 reduce
  272.4 0.6 reshape.135
  273.1 4.2 all-to-all-done.2
  277.3 3.3 all-to-all-start
  280.7 5.5 %all-to-all-done = bf16[8,2,512]{2,1,0:T(2,128)(2,1)S(1)} async-done(((bf16[8,2,512]{2,1,0:T(2,128)(2,1)}), bf16[8,2,512]{2,1,0:T(2,128)(2,1)S(1)}, u32[]{:S(2)}, u32[]{:S(2)}) %all-to-all-start) | async-done | bytes 16416 | tf_op jit(solution)/shard_map/all_to_all | solution.py:31
  286.2 0.6 reshape.136
  286.8 0.7 maximum_convert_fusion
  287.6 154.8 %reduce-scatter.2.cloned.1.call-done = bf16[1280,2048]{0,1:T(8,128)(2,1)} async-done(((bf16[5120,2048]{0,1:T(8,128)(2,1)}), bf16[1280,2048]{0,1:T(8,128)(2,1)}) %reduce-scatter.2.cloned.1.call-update) | async-done | bytes 5242896 | tf_op jit(solution)/shard_map/reduce_scatter | solution.py:73
  442.3 7.4 %fusion.31 = (f32[1280,1024]{0,1:T(8,128)}, f32[1280,1024]{0,1:T(8,128)}) fusion(bf16[1280,2048]{0,1:T(8,128)(2,1)} %reduce-scatter.2.cloned.1.call-done), kind=kLoop, calls=%fused_computation.47 | loop fusion | bytes 20971520 | tf_op jit(solution)/shard_map/slice | solution.py:82
  449.7 5.9 %copy.18 = f32[1280,1024]{1,0:T(8,128)} copy(f32[1280,1024]{0,1:T(8,128)} %get-tuple-element.14) | data formatting | bytes 10485760
  455.6 5.9 %copy.19 = f32[1280,1024]{1,0:T(8,128)} copy(f32[1280,1024]{0,1:T(8,128)} %get-tuple-element.13) | data formatting | bytes 10485760
  (9 shorter events, 0.1 us)
Async XLA Ops:
  7.2 247.9 %copy-start = (f32[8,1024]{1,0:T(8,128)S(1)}, f32[8,1024]{1,0:T(8,128)}, u32[]{:S(2)}) copy-start(f32[8,1024]{1,0:T(8,128)} %param.17) | copy-start | bytes 98308
  7.2 1.5 copy-start.4
  7.2 110.3 %all-gather.5.cloned.1.call-start = ((), (), s32[]{:S(2)}) async-start(), calls=%async_computation.5 | async-start | bytes 13107200 | tf_op jit(solution)/shard_map/all_gather | solution.py:62
  7.9 216.4 %all-gather.3.cloned.1.call-start = ((), (), s32[]{:S(2)}) async-start(), calls=%async_computation.4 | async-start | bytes 13107200 | tf_op jit(solution)/shard_map/all_gather | solution.py:67
  8.7 433.6 %reduce-scatter.2.cloned.1.call-start = ((), (), s32[]{:S(2)}) async-start(), calls=%async_computation.6 | async-start | bytes 26214400 | tf_op jit(solution)/shard_map/reduce_scatter | solution.py:73
  8.7 4.0 copy-start.1
  224.3 20.9 %slice-start = ((s8[10485760]{0:T(1024)(128)(4,1)}), s8[4194304]{0:T(1024)(128)(4,1)S(1)}, s32[]{:S(2)}) async-start(s8[10485760]{0:T(1024)(128)(4,1)} %bitcast.12), calls=%async_computation.7 | async-start | bytes 8388608
  224.3 20.9 %slice-start.1 = ((s8[10485760]{0:T(1024)(128)(4,1)}), s8[4194304]{0:T(1024)(128)(4,1)S(1)}, s32[]{:S(2)}) async-start(s8[10485760]{0:T(1024)(128)(4,1)} %bitcast.12), calls=%async_computation.8 | async-start | bytes 8388608
  236.2 9.0 %slice-start.2 = ((s8[10485760]{0:T(1024)(128)(4,1)}), s8[2097152]{0:T(1024)(128)(4,1)S(1)}, s32[]{:S(2)}) async-start(s8[10485760]{0:T(1024)(128)(4,1)} %bitcast.12), calls=%async_computation.9 | async-start | bytes 4194304
  254.4 0.7 copy-start.5
  254.4 1.2 copy-start.3
  254.4 9.6 %copy-start.2 = (bf16[8,1024]{1,0:T(8,128)(2,1)S(1)}, bf16[8,1024]{1,0:T(8,128)(2,1)}, u32[]{:S(2)}) copy-start(bf16[8,1024]{1,0:T(8,128)(2,1)} %param.16) | copy-start | bytes 49156
  258.1 10.3 %all-to-all-start.1 = ((bf16[8,2,512]{2,1,0:T(2,128)(2,1)}), bf16[8,2,512]{2,1,0:T(2,128)(2,1)S(1)}, u32[]{:S(2)}, u32[]{:S(2)}) async-start(bf16[8,2,512]{2,1,0:T(2,128)(2,1)} %reshape.139), calls=%async_computation.2 | async-start | bytes 32768 | tf_op jit(solution)/shard_map/all_to_all | solution.py:33
  268.3 8.9 %all-to-all-start.2 = ((bf16[8,2,512]{2,1,0:T(2,128)(2,1)}), bf16[8,2,512]{2,1,0:T(2,128)(2,1)S(1)}, u32[]{:S(2)}, u32[]{:S(2)}) async-start(bf16[8,2,512]{2,1,0:T(2,128)(2,1)} %reshape.137), calls=%async_computation.3 | async-start | bytes 32768 | tf_op jit(solution)/shard_map/all_to_all | solution.py:36
  277.3 8.9 %all-to-all-start = ((bf16[8,2,512]{2,1,0:T(2,128)(2,1)}), bf16[8,2,512]{2,1,0:T(2,128)(2,1)S(1)}, u32[]{:S(2)}, u32[]{:S(2)}) async-start(bf16[8,2,512]{2,1,0:T(2,128)(2,1)} %reshape.135), calls=%async_computation.1 | async-start | bytes 32768 | tf_op jit(solution)/shard_map/all_to_all | solution.py:31
Sparse Core Ops, SparseCore 0:
  9.8 107.6 all-gather.4
  119.4 104.9 all-gather.2
  254.5 187.7 reduce-scatter.1
where the time goes:
time: 469 us; the launch traced here: 468 us
  waiting for transfers between devices  358 us (76%)
  matrix products  42.5 us (9%)
  local copies, waits for them, and re-layouts  25.2 us (5%)
  other arithmetic  16.9 us (4%)
  between operations  13.9 us (3%)
  starting transfers between devices  11.4 us (2%)
    reduce_scatter x1, waiting for transfers between devices, per_device(): lax.psum_scatter(jnp.concatenate([outer_sum(left, grad_pre), outer_sum(ri...  155 us
    all_gather x1, waiting for transfers between devices, per_device(): lax.all_gather(up_weight, 'dp', axis=0, tiled=True)  103 us
    all_gather x1, waiting for transfers between devices, per_device(): lax.all_gather(down_weight, 'dp', axis=0, tiled=True)  85.2 us
    dot_general x2, matrix products, outer_sum(): lax.dot_general(left, right, (((0,), (0,)), ((), ())), preferred_element_...  20.7 us
    unnamed x26, local copies, waits for them, and re-layouts  15.6 us
    dot_general x1, matrix products, per_device(): jnp.dot(right, lax.all_gather(down_weight, 'dp', axis=0, tiled=True), pre...  11.9 us
    dot_general x1, matrix products, per_device(): jnp.dot(left, lax.all_gather(up_weight, 'dp', axis=0, tiled=True), prefer...  9.93 us
  transfers between devices with their start and end apart: 6, of which 6 were waited for; matrix products, arithmetic and copies ran while one was open for 7% of the time, Pallas kernels for 0%

commit v1 on v0

--- a/solution.py
+++ b/solution.py
@@ -4,6 +4,28 @@
 from jax.sharding import PartitionSpec as P
 
 EPS = 1e-06
+
+
+def joined_along(pieces, dim):
+    pieces = jnp.moveaxis(pieces, 0, dim)
+    shape = pieces.shape
+    return pieces.reshape(*shape[:dim], shape[dim] * shape[dim + 1], *shape[dim + 2 :])
+
+
+def gather_around(array, axis, dim):
+    length = lax.axis_size(axis)
+    pairs = [(i, (i + 1) % length) for i in range(length)]
+    back = [(b, a) for a, b in pairs]
+    lower, upper = ([], [])
+    for turn in range(length - 1):
+        if turn % 2 == 0:
+            lower.append(lax.ppermute(lower[-1] if lower else array, axis, pairs))
+        else:
+            upper.append(lax.ppermute(upper[-1] if upper else array, axis, back))
+    pieces = jnp.stack([*lower[::-1], array, *upper])
+    shift = lax.axis_index(axis) - len(lower)
+    pieces = pieces[(jnp.arange(length) - shift) % length]
+    return joined_along(pieces, dim)
 
 
 def normalize(tokens):
@@ -62,11 +84,7 @@
         lax.all_gather(up_weight, "dp", axis=0, tiled=True),
         preferred_element_type=jnp.float32,
     )
-    d_act = jnp.dot(
-        right,
-        lax.all_gather(down_weight, "dp", axis=0, tiled=True),
-        preferred_element_type=jnp.float32,
-    )
+    d_act = jnp.dot(right, gather_around(down_weight, "dp", 0), preferred_element_type=jnp.float32)
     act, grad_pre = gelu_pair(pre, d_act)
     left = normed
     right = masked

time: 469 us -> 574 us (1.22)
  waiting for transfers between devices: 358 us -> 414 us
  other arithmetic: 16.9 us -> 40.4 us
  local copies, waits for them, and re-layouts: 25.2 us -> 46 us
  starting transfers between devices: 11.4 us -> 18.2 us
    ppermute x0 -> x3, waiting for transfers between devices: none -> 245 us  [the longest x2 149 us: gather_around(): lower.append(lax.ppermute(lower[-1] if lower else array, axis, pairs))]
    all_gather x1, waiting for transfers between devices: 103 us -> 0.01 us  [per_device(): lax.all_gather(up_weight, 'dp', axis=0, tiled=True)]
    all_gather x1 -> x0, waiting for transfers between devices: 85.2 us -> none  [per_device(): lax.all_gather(down_weight, 'dp', axis=0, tiled=True)]
    gather x0 -> x3, local copies, waits for them, and re-layouts: none -> 20.8 us  [gather_around(): pieces = pieces[(jnp.arange(length) - shift) % length]]
    unnamed x1 -> x2, other arithmetic: 0.01 us -> 11.8 us
    another operation x0 -> x1, other arithmetic: none -> 7.32 us  [gather_around(): pieces = jnp.stack([*lower[::-1], array, *upper])]
    ppermute x0 -> x3, starting transfers between devices: none -> 6.42 us  [the longest x2 5.39 us: gather_around(): lower.append(lax.ppermute(lower[-1] if lower else array, axis, pairs))]
    unnamed x26 -> x24, local copies, waits for them, and re-layouts: 15.6 us -> 15.5 us
  transfers between devices with their start and end apart: 6 -> 8, of which waited for: 6 -> 7; matrix products, arithmetic and copies ran while one was open for 7% -> 9% of each run, Pallas kernels for 0% -> 0%
where the time goes in v1:
time: 574 us; the launch traced here: 572 us
  waiting for transfers between devices  414 us (72%)
  local copies, waits for them, and re-layouts  46 us (8%)
  other arithmetic  40.4 us (7%)
  matrix products  39.4 us (7%)
  starting transfers between devices  18.2 us (3%)
  between operations  14.2 us (2%)
    reduce_scatter x1, waiting for transfers between devices, per_device(): lax.psum_scatter(jnp.concatenate([outer_sum(left, grad_pre), outer_sum(ri...  155 us
    ppermute x2, waiting for transfers between devices, gather_around(): lower.append(lax.ppermute(lower[-1] if lower else array, axis, pairs))  149 us
    ppermute x1, waiting for transfers between devices, gather_around(): upper.append(lax.ppermute(upper[-1] if upper else array, axis, back))  95.8 us
    gather x3, local copies, waits for them, and re-layouts, gather_around(): pieces = pieces[(jnp.arange(length) - shift) % length]  20.8 us
    dot_general x2, matrix products, outer_sum(): lax.dot_general(left, right, (((0,), (0,)), ((), ())), preferred_element_...  17.4 us
    unnamed x24, local copies, waits for them, and re-layouts  15.5 us
    concatenate x1, other arithmetic, per_device(): jnp.concatenate([outer_sum(left, grad_pre), outer_sum(right, act)], axis=1)  12.8 us
    dot_general x1, matrix products, per_device(): jnp.dot(right, gather_around(down_weight, 'dp', 0), preferred_element_typ...  12.1 us
  transfers between devices with their start and end apart: 8, of which 7 were waited for; matrix products, arithmetic and copies ran while one was open for 9% of the time, Pallas kernels for 0%

profile of v1, /device:TPU:0, one launch (start us, length us, event | category | flops | bytes accessed | tf_op | source)
XLA Modules:
  0.0 572.4 jit_solution(4507546150809714010)
XLA Ops:
  7.2 0.0 copy-start
  7.2 0.0 all-gather.2.cloned.1.call-start
  7.2 0.7 all-gather.2.cloned.1.call-update
  7.9 0.0 reduce-scatter.2.cloned.1.call-start
  8.0 3.0 collective-permute-start
  11.0 1.0 collective-permute-start.2
  12.0 94.5 %collective-permute-done = bf16[1280,1024]{1,0:T(8,128)(2,1)S(1)} collective-permute-done((bf16[1280,1024]{1,0:T(8,128)(2,1)}, bf16[1280,1024]{1,0:T(8,128)(2,1)S(1)}, u32[]{:S(2)}, u32[]{:S(2)}) %collective-permute-start) | collective-permute-done | bytes 2621472 | tf_op jit(solution)/shard_map/ppermute | solution.py:22
  106.5 2.4 collective-permute-start.1
  108.9 0.7 convert_element_type.54
  109.6 0.0 copy-start.1
  109.6 0.0 copy-start.2
  109.6 3.4 convert_reduce_fusion
  113.0 0.6 copy-done.1
  113.6 1.5 fusion.2
  115.1 95.8 %collective-permute-done.2 = bf16[1280,1024]{1,0:T(8,128)(2,1)} collective-permute-done((bf16[1280,1024]{1,0:T(8,128)(2,1)}, bf16[1280,1024]{1,0:T(8,128)(2,1)}, u32[]{:S(2)}, u32[]{:S(2)}) %collective-permute-start.2) | collective-permute-done | bytes 2621472 | tf_op jit(solution)/shard_map/ppermute | solution.py:24
  210.9 54.8 %collective-permute-done.1 = bf16[1280,1024]{1,0:T(8,128)(2,1)} collective-permute-done((bf16[1280,1024]{1,0:T(8,128)(2,1)S(1)}, bf16[1280,1024]{1,0:T(8,128)(2,1)}, u32[]{:S(2)}, u32[]{:S(2)}) %collective-permute-start.1) | collective-permute-done | bytes 2621472 | tf_op jit(solution)/shard_map/ppermute | solution.py:22
  265.7 0.0 copy-done.2
  265.7 7.3 %pad_maximum_fusion.1 = bf16[4,1280,1024]{2,1,0:T(8,128)(2,1)} fusion(bf16[1,1280,1024]{2,1,0:T(8,128)(2,1)} %bitcast.3, bf16[1,1280,1024]{2,1,0:T(8,128)(2,1)S(1)} %bitcast.22, bf16[1,1280,1024]{2,1,0:T(8,128)(2,1)S(1)} %bitcast.23, bf16[1,1280,1024]{2,1,0:T(8,128)(2,1)} %bitcast), kind=kLoop, calls=%fused_computation.12 | loop fusion | flops 15728640 | bytes 20971520 | tf_op jit(solution)/shard_map/stack | solution.py:25
  273.1 9.4 %fusion.33 = (bf16[4,640,1024]{2,1,0:T(8,128)(2,1)}, bf16[4,640,1024]{2,1,0:T(8,128)(2,1)}) fusion(bf16[4,1280,1024]{2,1,0:T(8,128)(2,1)} %pad_maximum_fusion.1), kind=kLoop, calls=%fused_computation.58 | loop fusion | bytes 20971520 | tf_op jit(solution)/shard_map/gather | solution.py:27
  282.5 5.7 gather_fusion.1
  288.2 5.7 %gather_fusion.2 = bf16[4,640,1024]{2,1,0:T(8,128)(2,1)} fusion(bf16[4,640,1024]{2,1,0:T(8,128)(2,1)} %get-tuple-element.14, s32[1024]{0:T(1024)S(1)} %pad_clamp_fusion.1), kind=kCustom, calls=%fused_computation.4 | custom fusion | bytes 10485776 | tf_op jit(solution)/shard_map/gather | solution.py:27
  293.9 11.8 %pad_maximum_fusion.2 = bf16[4,1280,1024]{2,1,0:T(8,128)(2,1)} fusion(bf16[4,640,1024]{2,1,0:T(8,128)(2,1)} %gather_fusion.2, bf16[4,640,1024]{2,1,0:T(8,128)(2,1)} %gather_fusion.1), kind=kLoop, calls=%fused_computation.13 | loop fusion | flops 20971520 | bytes 20971520
  305.7 0.0 all-gather.2.cloned.1.call-done
  305.7 9.9 %fusion.31 = f32[512,1024]{1,0:T(8,128)S(1)} fusion(bf16[5120,1024]{1,0:T(8,128)(2,1)} %all-gather.2.cloned.1.call-done, bf16[512,5120]{1,0:T(8,128)(2,1)} %param.11, f32[512]{0:T(512)S(1)} %add_rsqrt_fusion, f32[512]{0:T(512)S(1)} %broadcast_multiply_fusion), kind=kOutput, calls=%fused_computation.57 | convolution fusion | flops 5379194880 | bytes 17829888 | tf_op jit(solution)/shard_map/dot_general | solution.py:82
  315.6 0.0 slice-start
  315.6 8.8 %convolution_convert_fusion = bf16[5120,1024]{0,1:T(8,128)(2,1)S(1)} fusion(bf16[512,5120]{1,0:T(8,128)(2,1)} %param.13, bf16[512]{0:T(512)(128)(2,1)S(1)} %convert_element_type.54, f32[512,1024]{1,0:T(8,128)S(1)} %fusion.31), kind=kOutput, calls=%fused_computation.14 | convolution fusion | flops 5381292032 | bytes 17826816 | tf_op jit(solution)/shard_map/dot_general | solution.py:44
  324.4 0.0 slice-start.1
  324.4 12.1 %fusion.15 = bf16[512,1024]{1,0:T(8,128)(2,1)S(1)} fusion(f32[512,1024]{1,0:T(8,128)S(1)} %fusion.31, bf16[5120,1024]{1,0:T(8,128)(2,1)} %bitcast.21, bf16[512,5120]{1,0:T(8,128)(2,1)} %param.13, bf16[512]{0:T(512)(128)(2,1)S(1)} %convert_element_type.54), kind=kOutput, calls=%fused_computation.29 | convolution fusion | flops 5381816320 | bytes 18875392 | tf_op jit(solution)/shard_map/dot_general | solution.py:87
  336.5 0.0 slice-done
  336.5 0.0 slice-done.1
  336.5 8.6 %convolution_convert_fusion.1 = bf16[5120,1024]{0,1:T(8,128)(2,1)} fusion(bf16[512,1024]{1,0:T(8,128)(2,1)S(1)} %fusion.15, bf16[512,5120]{1,0:T(8,128)(2,1)S(1)} %bitcast.20, f32[512]{0:T(512)S(1)} %add_rsqrt_fusion, f32[512]{0:T(512)S(1)} %broadcast_multiply_fusion), kind=kOutput, calls=%fused_computation.15 | convolution fusion | flops 5384437760 | bytes 16781312 | tf_op jit(solution)/shard_map/dot_general | solution.py:44
  345.1 12.8 %pad_maximum_fusion = bf16[5120,2048]{0,1:T(8,128)(2,1)} fusion(bf16[5120,1024]{0,1:T(8,128)(2,1)S(1)} %convolution_convert_fusion, bf16[5120,1024]{0,1:T(8,128)(2,1)} %convolution_convert_fusion.1), kind=kLoop, calls=%fused_computation.5 | loop fusion | flops 41943040 | bytes 41943040 | tf_op jit(solution)/shard_map/concatenate | solution.py:92
  357.9 0.0 copy-start.5
  357.9 0.0 copy-start.4
  357.9 0.0 copy-start.3
  357.9 0.0 reduce-scatter.2.cloned.1.call-update
  358.0 0.6 copy-done.5
  358.6 0.0 copy-done
  358.6 0.6 gather_fusion.3
  359.2 0.0 copy-done.4
  359.2 0.6 gather_fusion.4
  359.8 0.1 fusion.22
  359.9 0.5 broadcast.194
  360.4 0.7 reduce.1
  361.0 0.6 reshape.206
  361.6 5.1 all-to-all-start.2
  366.7 0.7 reduce.2
  367.4 0.6 reshape.208
  368.0 0.0 copy-done.3
  368.0 0.6 gather_fusion
  368.6 3.8 all-to-all-done.2
  372.4 3.3 all-to-all-start.1
  375.7 0.1 bitcast_select_fusion
  375.8 0.7 reduce
  376.5 0.6 reshape.204
  377.1 4.2 all-to-all-done.1
  381.3 3.3 all-to-all-start
  384.7 5.5 all-to-all-done
  390.2 0.6 reshape.205
  390.9 0.7 maximum_convert_fusion
  391.6 154.8 %reduce-scatter.2.cloned.1.call-done = bf16[1280,2048]{0,1:T(8,128)(2,1)} async-done(((bf16[5120,2048]{0,1:T(8,128)(2,1)}), bf16[1280,2048]{0,1:T(8,128)(2,1)}) %reduce-scatter.2.cloned.1.call-update) | async-done | bytes 5242896 | tf_op jit(solution)/shard_map/reduce_scatter | solution.py:91
  546.4 7.4 %fusion.34 = (f32[1280,1024]{0,1:T(8,128)}, f32[1280,1024]{0,1:T(8,128)}) fusion(bf16[1280,2048]{0,1:T(8,128)(2,1)} %reduce-scatter.2.cloned.1.call-done), kind=kLoop, calls=%fused_computation.59 | loop fusion | bytes 20971520 | tf_op jit(solution)/shard_map/slice | solution.py:100
  553.8 5.9 %copy.18 = f32[1280,1024]{1,0:T(8,128)} copy(f32[1280,1024]{0,1:T(8,128)} %get-tuple-element.16) | data formatting | bytes 10485760
  559.7 5.9 %copy.19 = f32[1280,1024]{1,0:T(8,128)} copy(f32[1280,1024]{0,1:T(8,128)} %get-tuple-element.15) | data formatting | bytes 10485760
  (10 shorter events, 0.1 us)
Async XLA Ops:
  7.2 351.4 %copy-start = (f32[8,1024]{1,0:T(8,128)S(1)}, f32[8,1024]{1,0:T(8,128)}, u32[]{:S(2)}) copy-start(f32[8,1024]{1,0:T(8,128)} %param.17) | copy-start | bytes 98308
  7.2 298.5 %all-gather.2.cloned.1.call-start = ((), (), s32[]{:S(2)}) async-start(), calls=%async_computation.4 | async-start | bytes 13107200 | tf_op jit(solution)/shard_map/all_gather | solution.py:84
  7.9 538.5 %reduce-scatter.2.cloned.1.call-start = ((), (), s32[]{:S(2)}) async-start(), calls=%async_computation.5 | async-start | bytes 26214400 | tf_op jit(solution)/shard_map/reduce_scatter | solution.py:91
  8.0 98.6 %collective-permute-start = (bf16[1280,1024]{1,0:T(8,128)(2,1)}, bf16[1280,1024]{1,0:T(8,128)(2,1)S(1)}, u32[]{:S(2)}, u32[]{:S(2)}) collective-permute-start(bf16[1280,1024]{1,0:T(8,128)(2,1)} %param.15), channel_id=1, source_target_pairs={{0,8},{8,16},{16,24},{24,0},{1,9},{9,17},{17,25},{25,1},{2,10},{10... | collective-permute-start | bytes 7864328 | tf_op jit(solution)/shard_map/ppermute | solution.py:22
  11.0 200.0 %collective-permute-start.2 = (bf16[1280,1024]{1,0:T(8,128)(2,1)}, bf16[1280,1024]{1,0:T(8,128)(2,1)}, u32[]{:S(2)}, u32[]{:S(2)}) collective-permute-start(bf16[1280,1024]{1,0:T(8,128)(2,1)} %param.15), channel_id=1, source_target_pairs={{8,0},{16,8},{24,16},{0,24},{9,1},{17,9},{25,17},{1,25},{10,2},{18... | collective-permute-start | bytes 7864328 | tf_op jit(solution)/shard_map/ppermute | solution.py:24
  106.5 159.2 %collective-permute-start.1 = (bf16[1280,1024]{1,0:T(8,128)(2,1)S(1)}, bf16[1280,1024]{1,0:T(8,128)(2,1)}, u32[]{:S(2)}, u32[]{:S(2)}) collective-permute-start(bf16[1280,1024]{1,0:T(8,128)(2,1)S(1)} %collective-permute-done), channel_id=1, source_target_pairs={{0,8},{8,16},{16,24},{24,0},{1,9},{9,17},{17,25},{25,1},{2,10},{10... | collective-permute-start | bytes 7864328 | tf_op jit(solution)/shard_map/ppermute | solution.py:22
  109.6 4.0 copy-start.1
  109.6 156.1 %copy-start.2 = (bf16[1280,1024]{1,0:T(8,128)(2,1)S(1)}, bf16[1280,1024]{1,0:T(8,128)(2,1)}, u32[]{:S(2)}) copy-start(bf16[1280,1024]{1,0:T(8,128)(2,1)} %param.15) | copy-start | bytes 7864324
  315.6 20.9 %slice-start = ((s8[5242880]{0:T(1024)(128)(4,1)}), s8[1048576]{0:T(1024)(128)(4,1)S(1)}, s32[]{:S(2)}) async-start(s8[5242880]{0:T(1024)(128)(4,1)} %bitcast.19), calls=%async_computation.6 | async-start | bytes 2097152
  324.4 12.1 %slice-start.1 = ((s8[5242880]{0:T(1024)(128)(4,1)}), s8[4194304]{0:T(1024)(128)(4,1)S(1)}, s32[]{:S(2)}) async-start(s8[5242880]{0:T(1024)(128)(4,1)} %bitcast.19), calls=%async_computation.7 | async-start | bytes 8388608
  357.9 0.7 copy-start.5
  357.9 1.2 copy-start.4
  357.9 10.1 %copy-start.3 = (bf16[8,1024]{1,0:T(8,128)(2,1)S(1)}, bf16[8,1024]{1,0:T(8,128)(2,1)}, u32[]{:S(2)}) copy-start(bf16[8,1024]{1,0:T(8,128)(2,1)} %param.16) | copy-start | bytes 49156
  361.6 10.7 %all-to-all-start.2 = ((bf16[8,2,512]{2,1,0:T(2,128)(2,1)}), bf16[8,2,512]{2,1,0:T(2,128)(2,1)S(1)}, u32[]{:S(2)}, u32[]{:S(2)}) async-start(bf16[8,2,512]{2,1,0:T(2,128)(2,1)} %reshape.206), calls=%async_computation.3 | async-start | bytes 32768 | tf_op jit(solution)/shard_map/all_to_all | solution.py:58
  372.4 8.9 %all-to-all-start.1 = ((bf16[8,2,512]{2,1,0:T(2,128)(2,1)}), bf16[8,2,512]{2,1,0:T(2,128)(2,1)S(1)}, u32[]{:S(2)}, u32[]{:S(2)}) async-start(bf16[8,2,512]{2,1,0:T(2,128)(2,1)} %reshape.208), calls=%async_computation.2 | async-start | bytes 32768 | tf_op jit(solution)/shard_map/all_to_all | solution.py:55
  381.3 8.9 %all-to-all-start = ((bf16[8,2,512]{2,1,0:T(2,128)(2,1)}), bf16[8,2,512]{2,1,0:T(2,128)(2,1)S(1)}, u32[]{:S(2)}, u32[]{:S(2)}) async-start(bf16[8,2,512]{2,1,0:T(2,128)(2,1)} %reshape.204), calls=%async_computation.1 | async-start | bytes 32768 | tf_op jit(solution)/shard_map/all_to_all | solution.py:53
Sparse Core Ops, SparseCore 0:
  9.8 191.6 all-gather.1
  358.1 188.2 reduce-scatter.1
